TPU v7x, 32 devices: a whole 2x2x4 slice. The times are simulated.
32 devices in a mesh: grp: 2 (over x), tok: 8 (over z, y), side: 2 (over core).
Axes of the slice: x: 2, y: 2, z: 4, core: 2. Of those that a mesh axis runs over, the one named last changes fastest.
Arguments:
- hidden_in: bfloat16 [512, 3072], P(('grp', 'tok')), parts along dimension 0, may hold values from -6 to 6
- queries: bfloat16 [512, 24, 128], P(('grp', 'tok'), 'side'), parts along dimension 0, may hold values from -32 to 32
- key_new: bfloat16 [512, 4, 128], P(('grp', 'tok'), 'side'), parts along dimension 0, may hold values from -32 to 32
- value_new: bfloat16 [512, 4, 128], P(('grp', 'tok'), 'side'), parts along dimension 0, may hold values from -6 to 6
- cache_keys: bfloat16 [512, 4, 128, 128], P(('grp', 'tok'), 'side'), parts along dimension 0, may hold values from -32 to 32
- cache_values: bfloat16 [512, 4, 128, 128], P(('grp', 'tok'), 'side'), parts along dimension 0, may hold values from -6 to 6
- lengths: int32 [512], P(('grp', 'tok')), parts along dimension 0, may hold values from 1 to 128, 16384 in all
- out_weight: bfloat16 [3072, 3072], P('side', 'tok'), may hold values from -0.109375 to 0.109375
- norm_gain: float32 [3072], replicated, may hold values from 0.1 to 1.9
- router_weight: float32 [3072, 4], replicated, may hold values from -0.109375 to 0.109375
- gate_weight: bfloat16 [3072, 32768], P(None, ('tok', 'side')), may hold values from -0.109375 to 0.109375
- up_weight: bfloat16 [3072, 32768], P(None, ('tok', 'side')), may hold values from -0.109375 to 0.109375
- down_weight: bfloat16 [32768, 3072], P(('tok', 'side')), may hold values from -0.0625 to 0.0625
- routes: int32 [512, 2], P('grp'), parts along dimension 0, may hold values from 0 to 3, all different within a row; in each aligned block of 32 rows (0 to 31, 32 to 63, ...) at most 24 rows name the same one
Outputs:
- mixed: bfloat16 [512, 3072], P(('grp', 'tok')), parts along dimension 0
There are 2 independent parts, one for each index of `grp`. A program takes and returns all parts, laid end to end along the dimension named above; an argument that names none is the same for every part. Nothing has to cross between parts.
Inputs may be any that keep to these rules, and one draw needn't show every extreme that they name: Every sequence has at least one valid cache position and some sequence has 128; in each serving group the lengths sum to 16384. `routes`: each row names two different experts; among the rows of one index of tok (aligned blocks of 32 rows) no expert is named by more than 24 rows, and some expert reaches 24 in some block.
All inputs are finite; a program needn't handle non-finite values.
Results may differ from a plain program's by a relative error of at most 0.0075.
Values may be sent and summed in bfloat16 or wider, within the bound.
A program may use at most 128 MiB of HBM per device.

v0:
```python
import functools
import math

import jax
import jax.numpy as jnp
from jax import lax
from jax.experimental import pallas as pl
from jax.experimental.pallas import tpu as pltpu
from jax.sharding import PartitionSpec as P

CAP = 24
PIECES = 4
HIDDEN_TILE = 512
STRIPS = 2


def attend(queries, key_new, value_new, cache_keys, cache_values, lengths):
    seq_count, head_count, head_width = queries.shape
    kv_count = key_new.shape[1]
    places = cache_keys.shape[2]
    scaling = 1.0 / math.sqrt(head_width)
    grouped = queries.reshape(seq_count, kv_count, head_count // kv_count, head_width)
    scores = (
        jnp.einsum("skgd,skpd->skgp", grouped, cache_keys, preferred_element_type=jnp.float32)
        * scaling
    )
    usable = jnp.arange(places, dtype=jnp.int32)[None, :] < lengths[:, None]
    scores = jnp.where(usable[:, None, None, :], scores, -jnp.inf)
    own_score = (
        jnp.einsum("skgd,skd->skg", grouped, key_new, preferred_element_type=jnp.float32) * scaling
    )
    top_score = jnp.maximum(jnp.max(scores, axis=-1), own_score)
    weights = jnp.exp(scores - top_score[..., None])
    own_weight = jnp.exp(own_score - top_score)
    totals = jnp.sum(weights, axis=-1) + own_weight
    prob_low = (weights / totals[..., None]).astype(jnp.bfloat16)
    own_low = (own_weight / totals).astype(jnp.bfloat16)
    mixture = jnp.einsum(
        "skgp,skpd->skgd", prob_low, cache_values, preferred_element_type=jnp.float32
    )
    mixture = (
        mixture
        + own_low.astype(jnp.float32)[..., None] * value_new.astype(jnp.float32)[:, :, None, :]
    )
    return mixture.astype(jnp.bfloat16).reshape(seq_count, head_count * head_width)

def wire(block):
    rows, width = block.shape
    extra = rows - 16
    half = width // 2
    tail = jnp.concatenate([block[16:, :half], block[16:, half:]], axis=0)
    return jnp.concatenate([block[:16], tail], axis=1).astype(jnp.bfloat16)


def unwire(block, width):
    half = width // 2
    full = block.astype(jnp.float32)
    tail = jnp.concatenate([full[:8, width:], full[8:, width:]], axis=1)
    return jnp.concatenate([full[:, :width], tail], axis=0)


def body(
    dims,
    attn_ref,
    hidden_ref,
    routes_t_ref,
    gain_ref,
    router_ref,
    out_hbm,
    gate_hbm,
    up_hbm,
    down_hbm,
    out_ref,
    heads,
    proj,
    proj_peer,
    cols,
    cols_in,
    stream_buf,
    tokens,
    packed,
    active,
    out_w,
    gate_w,
    up_w,
    down_w,
    mine,
    theirs,
    theirs_in,
    y_out,
    y_in,
    z_out,
    z_in,
    final,
    w_sem,
    ag_zs,
    ag_zr,
    ag_ys,
    ag_yr,
    tok_s,
    tok_r,
    col_s,
    col_r,
    one_s,
    one_r,
    rz_s,
    rz_r,
    ry_s,
    ry_r,
):
    T, Z, R, rows, cap = dims
    half_rows = rows // 2
    D = hidden_ref.shape[1]
    half_d = D // 2
    total = T * rows
    slots = T * cap
    part = Z * cap
    hid = gate_w.shape[1]
    tok = lax.axis_index("tok")
    side = lax.axis_index("side")
    z = tok // R
    r = tok % R
    other = 1 - side

    def zo(d):
        return (z + d) % Z

    def ro(d):
        return (r + d) % R

    def copy(src, dst, ssem, rsem, t=None, s=None):
        where = {"tok": tok if t is None else t, "side": side if s is None else s}
        return pltpu.make_async_remote_copy(
            src_ref=src,
            dst_ref=dst,
            send_sem=ssem,
            recv_sem=rsem,
            device_id=where,
            device_id_type=pl.DeviceIdType.MESH,
        )

    loads = [
        pltpu.make_async_copy(out_hbm, out_w, w_sem.at[3]),
        pltpu.make_async_copy(gate_hbm, gate_w, w_sem.at[0]),
        pltpu.make_async_copy(up_hbm, up_w, w_sem.at[1]),
        pltpu.make_async_copy(down_hbm, down_w, w_sem.at[2]),
    ]
    for load in loads:
        load.start()

    heads[pl.ds(pl.multiple_of(tok * rows, rows), rows), :] = attn_ref[...]
    barrier = pltpu.get_barrier_semaphore()
    for d in range(1, T):
        pl.semaphore_signal(
            barrier,
            inc=1,
            device_id={"tok": (tok + d) % T, "side": side},
            device_id_type=pl.DeviceIdType.MESH,
        )
    pl.semaphore_signal(
        barrier, inc=1, device_id={"tok": tok, "side": other}, device_id_type=pl.DeviceIdType.MESH
    )
    pl.semaphore_wait(barrier, T)

    pending = []

    def gather(phase, slot, landed):
        def along(zs, hop, way, piece):
            k = (phase, hop, (way + 1) // 2, piece)
            here = slot(zs * R + r, piece)
            return copy(here, here, ag_zs.at[k], ag_zr.at[k], t=(z + way) * R + r)

        def landing(zs, hop, way, piece):
            k = (phase, hop, (way + 1) // 2, piece)
            here = slot(zs * R + r, piece)
            return copy(here, here, ag_zs.at[k], ag_zr.at[k], t=tok)

        def across(zs, piece):
            for e in range(1, R):
                k = (phase, e, zs, piece)
                here = slot(zs * R + r, piece)
                c = copy(here, here, ag_ys.at[k], ag_yr.at[k], t=z * R + ro(e))
                c.start()

        def crossed(zs, piece):
            for e in range(1, R):
                k = (phase, e, zs, piece)
                here = slot(zs * R + ro(R - e), piece)
                copy(here, here, ag_ys.at[k], ag_yr.at[k], t=z * R + ro(e)).wait_recv()
                landed(zs * R + ro(R - e), piece)

        def send_on(zs, hop, way, piece):
            ok = (z + way >= 0) & (z + way < Z)

            @pl.when(ok)
            def _():
                along(zs, hop, way, piece).start()

        for piece in range(PIECES):
            for way in (1, -1):
                send_on(z, 0, way, piece)
            across(z, piece)
        for hop in range(1, Z):
            for piece in range(PIECES):
                for way in (1, -1):
                    zs = z - way * hop

                    @pl.when((zs >= 0) & (zs < Z))
                    def _(zs=zs, way=way, piece=piece, hop=hop):
                        landing(zs, hop - 1, way, piece).wait_recv()
                        if hop < Z - 1:
                            send_on(zs, hop, way, piece)
                        across(zs, piece)
                        landed(zs * R + r, piece)

            for piece in range(PIECES):
                if hop == 1:
                    crossed(z, piece)
                else:
                    for way in (1, -1):
                        zs = z - way * (hop - 1)

                        @pl.when((zs >= 0) & (zs < Z))
                        def _(zs=zs, piece=piece):
                            crossed(zs, piece)

        for piece in range(PIECES):
            for way in (1, -1):
                zs = z - way * (Z - 1)

                @pl.when((zs >= 0) & (zs < Z))
                def _(zs=zs, piece=piece):
                    crossed(zs, piece)

    def settle(phase, slot):
        for piece in range(PIECES):
            for zs in range(Z):
                for e in range(1, R):
                    k = (phase, e, zs, piece)
                    here = slot(zs * R + r, piece)
                    copy(here, here, ag_ys.at[k], ag_yr.at[k], t=z * R + ro(e)).wait_send()
            for hop in range(Z - 1):
                for way in (1, -1):
                    zs = z - way * hop
                    ok = (zs >= 0) & (zs < Z) & (z + way >= 0) & (z + way < Z)

                    @pl.when(ok)
                    def _(zs=zs, hop=hop, way=way, piece=piece):
                        k = (phase, hop, (way + 1) // 2, piece)
                        here = slot(zs * R + r, piece)
                        copy(
                            here, here, ag_zs.at[k], ag_zr.at[k], t=(z + way) * R + r
                        ).wait_send()

    head_piece = heads.shape[1] // PIECES

    def head_slot(t, piece):
        return heads.at[
            pl.ds(pl.multiple_of(t * rows, rows), rows), pl.ds(piece * head_piece, head_piece)
        ]

    gather(0, head_slot, lambda holder, piece: None)
    loads[0].wait()

    width = out_w.shape[1]
    p = jnp.dot(heads[...], out_w[...], preferred_element_type=jnp.float32)
    proj[...] = p.reshape(T, 2, half_rows, width)
    c = copy(proj.at[:, other], proj_peer, one_s.at[0], one_r.at[0], s=other)
    c.start()
    pending.append(c)
    c.wait_recv()
    cols[...] = (proj[:, side] + proj_peer[...]).astype(jnp.bfloat16)
    for d in range(1, T):
        t = (tok + d) % T
        c = copy(cols.at[t], cols_in.at[tok], col_s.at[d], col_r.at[d], t=t)
        c.start()
        pending.append(c)
    cols_in[tok] = cols[tok]
    for d in range(1, T):
        t = (tok + T - d) % T
        copy(cols.at[t], cols_in.at[t], col_s.at[d], col_r.at[d], t=t).wait_recv()

    my_rows = pl.multiple_of(side * half_rows, half_rows)
    projected = jnp.concatenate([cols_in[t].astype(jnp.float32) for t in range(T)], axis=1)
    low = (hidden_ref[pl.ds(my_rows, half_rows), :].astype(jnp.float32) + projected).astype(
        jnp.bfloat16
    )
    stream_buf[pl.ds(my_rows, half_rows), :] = low
    stream = low.astype(jnp.float32)
    normed = (
        stream
        * lax.rsqrt(jnp.mean(stream * stream, axis=-1, keepdims=True) + 1e-05)
        * gain_ref[...]
    ).astype(jnp.bfloat16)

    token_piece = D // PIECES

    def token_slot(t, piece, s=None):
        s = side if s is None else s
        return tokens.at[
            pl.ds(pl.multiple_of(t * rows + s * half_rows, half_rows), half_rows),
            pl.ds(piece * token_piece, token_piece),
        ]

    tokens[pl.ds(pl.multiple_of(tok * rows + side * half_rows, half_rows), half_rows), :] = normed

    def over(holder, piece, s=None):
        here = token_slot(holder, piece, s)
        return copy(here, here, tok_s.at[holder, piece], tok_r.at[holder, piece], s=other)

    expert = z
    lanes = lax.broadcasted_iota(jnp.int32, (1, total), 1)
    block = lax.div(lanes, rows)
    hit = (routes_t_ref[0:1, :] == expert) | (routes_t_ref[1:2, :] == expert)
    row_i = lax.broadcasted_iota(jnp.int32, (total, total), 0)
    col_i = lax.broadcasted_iota(jnp.int32, (total, total), 1)
    before = (row_i < col_i) & (lax.div(row_i, rows) == lax.div(col_i, rows))
    hits = jnp.broadcast_to(jnp.where(hit, 1.0, 0.0), (8, total)).astype(jnp.bfloat16)
    rank = jnp.dot(
        hits,
        jnp.where(before, 1.0, 0.0).astype(jnp.bfloat16),
        preferred_element_type=jnp.float32,
    )[0:1].astype(jnp.int32)
    base = (lax.rem(block, R) * Z + lax.div(block, R)) * cap
    place = jnp.where(hit & (rank < cap), base + rank, -1)
    slot_i = lax.broadcasted_iota(jnp.int32, (slots, total), 0)
    put = jnp.where(slot_i == place, 1.0, 0.0).astype(jnp.bfloat16)

    for piece in range(PIECES):
        over(tok, piece).start()
    c = copy(
        stream_buf.at[pl.ds(my_rows, half_rows)],
        stream_buf.at[pl.ds(my_rows, half_rows)],
        one_s.at[1],
        one_r.at[1],
        s=other,
    )
    c.start()
    pending.append(c)
    gather(1, token_slot, lambda holder, piece: over(holder, piece).start())
    for t in range(T):
        for piece in range(PIECES):
            over(t, piece, other).wait_recv()

    @pl.loop(0, D // 512)
    def _(i):
        here = pl.ds(pl.multiple_of(i * 512, 512), 512)
        packed[:, here] = jnp.dot(
            put, tokens[:, here], preferred_element_type=jnp.float32
        ).astype(jnp.bfloat16)

    loads[1].wait()
    loads[2].wait()

    tile = min(HIDDEN_TILE, hid)

    @pl.loop(0, hid // tile)
    def _(i):
        here = pl.ds(pl.multiple_of(i * tile, tile), tile)
        g = jnp.dot(packed[...], gate_w[:, here], preferred_element_type=jnp.float32)
        u = jnp.dot(packed[...], up_w[:, here], preferred_element_type=jnp.float32)
        active[:, here] = (g / (1.0 + jnp.exp(-g)) * u).astype(jnp.bfloat16)

    loads[3].wait()

    strip = half_d // STRIPS
    far_up = z < Z // 2

    def down(start, q):
        at = pl.ds(pl.multiple_of(start * half_d + q * strip, 128), strip)
        return jnp.dot(active[...], down_w[:, at], preferred_element_type=jnp.float32)

    def y_copy(q, e, k):
        i = (q, e, k)
        return copy(y_out.at[i], y_in.at[i], ry_s.at[i], ry_r.at[i], t=z * R + ro(e))

    def cores_copy(q):
        return copy(theirs.at[q], theirs_in.at[q], one_s.at[q + 4], one_r.at[q + 4], s=other)

    for q in range(STRIPS):
        theirs[q] = down(other, q).astype(jnp.bfloat16)
        cores_copy(q).start()
        mine[q] = down(side, q)
        cores_copy(q).wait_recv()
        mine[q] = mine[q] + theirs_in[q].astype(jnp.float32)
        for k in range(Z):
            to = jnp.where(far_up, Z - 1 - k, k)
            for e in range(1, R):
                at = pl.multiple_of(ro(e) * part + to * cap, 8)
                y_out[q, e, k] = wire(mine[q, pl.ds(at, cap), :])
                y_copy(q, e, k).start()
    for q in range(STRIPS):
        for k in range(Z):
            to = jnp.where(far_up, Z - 1 - k, k)
            at = pl.multiple_of(r * part + to * cap, 8)
            total_rows = mine[q, pl.ds(at, cap), :]
            for e in range(1, R):
                y_copy(q, e, k).wait_recv()
                total_rows = total_rows + unwire(y_in[q, e, k], strip)
            z_out[q, to] = wire(total_rows)

            @pl.when(to == z)
            def _(to=to, q=q):
                z_in[q, z] = z_out[q, to]

            @pl.when(to != z)
            def _(to=to, q=q):
                copy(
                    z_out.at[q, to], z_in.at[q, z], rz_s.at[q, to], rz_r.at[q, z], t=to * R + r
                ).start()

    own = pl.ds(pl.multiple_of(tok * rows, rows), rows)
    mine_now = tokens[own, :].astype(jnp.float32)
    lane_t = lax.broadcasted_iota(jnp.int32, (rows, total), 1)
    row_t = lax.broadcasted_iota(jnp.int32, (rows, total), 0)
    at_own = lane_t == tok * rows + row_t

    def own_route(k):
        return jnp.sum(jnp.where(at_own, routes_t_ref[k : k + 1, :], 0), axis=1, keepdims=True)

    r0, r1 = own_route(0), own_route(1)
    lane = lax.broadcasted_iota(jnp.int32, (rows, 128), 1)
    l0 = jnp.zeros((rows, 1), jnp.float32)
    l1 = jnp.zeros((rows, 1), jnp.float32)
    for k in range(Z):
        logit = jnp.sum(mine_now * router_ref[k : k + 1, :], axis=1, keepdims=True)
        l0 = jnp.where(r0 == k, logit, l0)
        l1 = jnp.where(r1 == k, logit, l1)
    g0 = 1.0 / (1.0 + jnp.exp(l1 - l0))
    g1 = 1.0 - g0
    both = jnp.where((lane == r0) | (lane == r1), 1.0, 0.0).astype(jnp.bfloat16)
    row_n = lax.broadcasted_iota(jnp.int32, (rows, rows), 0)
    col_n = lax.broadcasted_iota(jnp.int32, (rows, rows), 1)
    ranks = jnp.dot(
        jnp.where(col_n < row_n, 1.0, 0.0).astype(jnp.bfloat16),
        both,
        preferred_element_type=jnp.float32,
    ).astype(jnp.int32)
    at = lax.broadcasted_iota(jnp.int32, (rows, part), 1)

    def find(k):
        rank = jnp.sum(jnp.where(lane == k, ranks, 0), axis=1, keepdims=True)
        return jnp.where(at == k * cap + rank, 1.0, 0.0).astype(jnp.bfloat16)

    pick0, pick1 = find(r0), find(r1)

    copy(
        stream_buf.at[pl.ds(my_rows, half_rows)],
        stream_buf.at[pl.ds(pl.multiple_of(other * half_rows, half_rows), half_rows)],
        one_s.at[1],
        one_r.at[1],
        s=other,
    ).wait_recv()
    strips = []
    for q in range(STRIPS):
        for d in range(1, Z):
            src = zo(d)
            here = z_in.at[q, src]
            copy(here, here, rz_s.at[q, src], rz_r.at[q, src], t=src * R + r).wait_recv()
        got = jnp.concatenate([unwire(z_in[q, e], strip) for e in range(Z)], axis=0)
        got = got.astype(jnp.bfloat16)
        strips.append(
            g0 * jnp.dot(pick0, got, preferred_element_type=jnp.float32)
            + g1 * jnp.dot(pick1, got, preferred_element_type=jnp.float32)
        )
    half = pl.ds(pl.multiple_of(side * half_d, half_d), half_d)
    mixed = stream_buf[:, half].astype(jnp.float32) + jnp.concatenate(strips, axis=1)
    final[side] = mixed.astype(jnp.bfloat16)
    c = copy(final.at[side], final.at[side], one_s.at[3], one_r.at[3], s=other)
    c.start()
    pending.append(c)
    copy(final.at[other], final.at[other], one_s.at[3], one_r.at[3], s=other).wait_recv()
    out_ref[:, :half_d] = final[0]
    out_ref[:, half_d:] = final[1]
    for c in pending:
        c.wait_send()
    for q in range(STRIPS):
        cores_copy(q).wait_send()
        for e in range(1, R):
            for k in range(Z):
                y_copy(q, e, k).wait_send()
        for d in range(1, Z):
            to = zo(d)
            copy(
                z_out.at[q, to], z_in.at[q, z], rz_s.at[q, to], rz_r.at[q, z], t=to * R + r
            ).wait_send()
    settle(0, head_slot)
    settle(1, token_slot)
    for t in range(T):
        for piece in range(PIECES):
            over(t, piece).wait_send()


def local(
    hidden_in,
    queries,
    key_new,
    value_new,
    cache_keys,
    cache_values,
    lengths,
    out_weight,
    norm_gain,
    router_weight,
    gate_weight,
    up_weight,
    down_weight,
    routes,
):
    rows, D = hidden_in.shape
    T = lax.axis_size("tok")
    Z = router_weight.shape[1]
    R = T // Z
    cap = min(CAP, rows)
    hid = gate_weight.shape[1]
    width = out_weight.shape[1]
    bf, f32 = jnp.bfloat16, jnp.float32
    attn_out = attend(queries, key_new, value_new, cache_keys, cache_values, lengths)
    half_d = D // 2
    strip = half_d // STRIPS
    wire_width = strip * cap // 16
    dma = pltpu.SemaphoreType.DMA
    vmem = pl.BlockSpec(memory_space=pltpu.VMEM)
    anyspace = pl.BlockSpec(memory_space=pl.ANY)
    return pl.pallas_call(
        functools.partial(body, (T, Z, R, rows, cap)),
        out_shape=jax.ShapeDtypeStruct((rows, D), bf),
        in_specs=[vmem] * 5 + [anyspace] * 4,
        out_specs=vmem,
        scratch_shapes=[
            pltpu.VMEM((T * rows, attn_out.shape[1]), bf),
            pltpu.VMEM((T, 2, rows // 2, width), f32),
            pltpu.VMEM((T, rows // 2, width), f32),
            pltpu.VMEM((T, rows // 2, width), bf),
            pltpu.VMEM((T, rows // 2, width), bf),
            pltpu.VMEM((rows, D), bf),
            pltpu.VMEM((T * rows, D), bf),
            pltpu.VMEM((T * cap, D), bf),
            pltpu.VMEM((T * cap, hid), bf),
            pltpu.VMEM(out_weight.shape, bf),
            pltpu.VMEM(gate_weight.shape, bf),
            pltpu.VMEM(up_weight.shape, bf),
            pltpu.VMEM(down_weight.shape, bf),
            pltpu.VMEM((STRIPS, T * cap, strip), f32),
            pltpu.VMEM((STRIPS, T * cap, strip), bf),
            pltpu.VMEM((STRIPS, T * cap, strip), bf),
            pltpu.VMEM((STRIPS, R, Z, 16, wire_width), bf),
            pltpu.VMEM((STRIPS, R, Z, 16, wire_width), bf),
            pltpu.VMEM((STRIPS, Z, 16, wire_width), bf),
            pltpu.VMEM((STRIPS, Z, 16, wire_width), bf),
            pltpu.VMEM((2, rows, half_d), bf),
            dma((4,)),
            dma((2, Z - 1, 2, PIECES)),
            dma((2, Z - 1, 2, PIECES)),
            dma((2, R, Z, PIECES)),
            dma((2, R, Z, PIECES)),
            dma((T, PIECES)),
            dma((T, PIECES)),
            dma((T,)),
            dma((T,)),
            dma((4 + STRIPS,)),
            dma((4 + STRIPS,)),
            dma((STRIPS, Z)),
            dma((STRIPS, Z)),
            dma((STRIPS, R, Z)),
            dma((STRIPS, R, Z)),
        ],
        compiler_params=pltpu.CompilerParams(
            collective_id=0, has_side_effects=True, vmem_limit_bytes=67043328
        ),
    )(
        attn_out,
        hidden_in,
        routes.T,
        norm_gain.reshape(1, D),
        router_weight.T,
        out_weight,
        gate_weight,
        up_weight,
        down_weight,
    )


def solution(mesh):
    return jax.shard_map(
        local,
        mesh=mesh,
        in_specs=(
            P(("grp", "tok"), None),
            P(("grp", "tok"), "side", None),
            P(("grp", "tok"), "side", None),
            P(("grp", "tok"), "side", None),
            P(("grp", "tok"), "side", None, None),
            P(("grp", "tok"), "side", None, None),
            P(("grp", "tok")),
            P("side", "tok"),
            P(),
            P(),
            P(None, ("tok", "side")),
            P(None, ("tok", "side")),
            P(("tok", "side"), None),
            P("grp", None),
        ),
        out_specs=P(("grp", "tok"), None),
        check_vma=False,
    )
```

profile of v0, /device:TPU:0, one launch (start us, length us, event | category | flops | bytes accessed | tf_op | source)
XLA Modules:
  0.0 71.9 jit_solution(683589956598218466)
XLA Ops:
  0.0 0.0 copy-start
  0.0 0.9 %iota_compare_fusion = pred[32,128]{1,0:T(8,128)(4,1)S(1)} fusion(s32[32]{0:T(128)} %param.20), kind=kLoop, calls=%fused_computation.16 | loop fusion | flops 4096 | bytes 4224 | tf_op jit(solution)/shard_map/lt | solution.py:27
  0.9 1.1 %fusion.3 = f32[32,2,1,6]{3,2,1,0:T(1,128)S(1)} fusion(bf16[32,2,6,128]{3,0,2,1:T(8,128)(2,1)} %bitcast.9, bf16[32,2,128,1]{2,1,0,3:T(2,128)(2,1)} %bitcast.16), kind=kOutput, calls=%fused_computation.7 | convolution fusion | flops 98304 | bytes 116224 | tf_op jit(solution)/shard_map/skgd,skd->skg/dot_general | solution.py:30
  2.0 0.7 %convert_element_type.18 = f32[32,2,128]{2,1,0:T(2,128)S(1)} convert(bf16[32,2,128]{2,1,0:T(2,128)(2,1)} %param.17) | non-fusion elementwise | flops 8192 | bytes 49152 | tf_op jit(solution)/shard_map/convert_element_type | solution.py:43
  2.7 2.9 %fusion.11 = (f32[32,2,6]{2,1,0:T(2,128)S(1)}, f32[32,2,6,128]{3,2,1,0:T(8,128)S(1)}) fusion(bf16[32,2,128,128]{3,2,1,0:T(8,128)(2,1)} %param.18, bf16[32,2,6,128]{3,0,2,1:T(8,128)(2,1)} %bitcast.10, pred[32,128]{1,0:T(8,128)(4,1)S(1)} %iota_compare_fusion), kind=kOutput, calls=%fused_computation.19 | convolution fusion | flops 12729984 | bytes 2397696 | tf_op jit(solution)/shard_map/skgd,skpd->skgp/dot_general | solution.py:24
  5.7 0.3 fusion.2
  6.0 0.1 fusion.10
  6.0 0.0 copy-done
  6.1 0.7 %fusion.1 = bf16[32,2,6,128]{3,2,1,0:T(8,128)(2,1)S(1)} fusion(bf16[32,2,128,128]{3,2,1,0:T(8,128)(2,1)S(1)} %copy-done, f32[32,2,6,128]{3,2,1,0:T(8,128)S(1)} %get-tuple-element.8, f32[32,2,128]{2,1,0:T(2,128)S(1)} %convert_element_type.18, f32[32,2,6]{2,1,0:T(2,128)S(1)} %get-tuple-element.6, f32[32,2,6]{2,1,0:T(2,128)S(1)} %get-tuple-element.5, ...), kind=kOutput, calls=%fused_computation.3 | convolution fusion | flops 12877824 | bytes 2429440 | tf_op jit(solution)/shard_map/skgp,skpd->skgd/dot_general | solution.py:38
  6.8 0.8 %reshape.31.attn_ref = bf16[32,1536]{1,0:T(8,128)(2,1)} reshape(bf16[32,2,6,128]{3,2,1,0:T(8,128)(2,1)S(1)} %fusion.1) | data formatting | bytes 196608 | tf_op jit(solution)/shard_map/reshape | solution.py:45
  7.6 62.7 %shard_map.136 = bf16[32,3072]{1,0:T(8,128)(2,1)} custom-call(bf16[32,1536]{1,0:T(8,128)(2,1)} %reshape.31.attn_ref, bf16[32,3072]{1,0:T(8,128)(2,1)} %hidden_ref.1, s32[2,256]{1,0:T(2,128)} %bitcast.15, f32[1,3072]{1,0:T(1,128)} %bitcast.14, f32[4,3072]{1,0:T(4,128)} %bitcast.13, bf16[1536,384]{1,0:T(8,128)(2,1)} %out_hbm.1, bf16[3072,2048]{1,0:T(8,128)(2,1)} %gate_hbm.1, ...), custom_call_target="tpu_custom_call" | custom-call | tf_op jit(solution)/shard_map/pallas_call | solution.py:525
  70.3 1.6 %copy.28 = bf16[32,3072]{1,0:T(8,128)(2,1)} copy(bf16[32,3072]{1,0:T(8,128)(2,1)} %shard_map.136) | data formatting | bytes 393216
  (1 shorter events, 0.0 us)
Async XLA Ops:
  0.0 6.0 %copy-start = (bf16[32,2,128,128]{3,2,1,0:T(8,128)(2,1)S(1)}, bf16[32,2,128,128]{3,2,1,0:T(8,128)(2,1)}, u32[]{:S(2)}) copy-start(bf16[32,2,128,128]{3,2,1,0:T(8,128)(2,1)} %param.19) | copy-start | bytes 6291460
where the time goes:
time: 72.2 us; the launch traced here: 71.9 us
  Pallas kernels  62.7 us (87%)
  matrix products  4.77 us (7%)
  local copies, waits for them, and re-layouts  2.39 us (3%)
  other arithmetic  1.96 us (3%)
    pallas_call x1, Pallas kernels, local(): pl.pallas_call(functools.partial(body, (T, Z, R, rows, cap)), out_shape=j...  62.7 us
    dot_general x1, matrix products, attend(): jnp.einsum('skgd,skpd->skgp', grouped, cache_keys, preferred_element_type...  2.95 us
    unnamed x3, local copies, waits for them, and re-layouts  1.62 us

commit v1 on v0

v1 whole, which is shorter than its diff:
```python
import functools
import math

import jax
import jax.numpy as jnp
from jax import lax
from jax.experimental import pallas as pl
from jax.experimental.pallas import tpu as pltpu
from jax.sharding import PartitionSpec as P

CAP = 24
HIDDEN_TILE = 512
STRIPS = 3
GROUP = 16
CHUNK = 8

bf, f32, i32 = jnp.bfloat16, jnp.float32, jnp.int32


def wire(block):
    rows, width = block.shape
    half = width // 2
    tail = jnp.concatenate([block[16:, :half], block[16:, half:]], axis=0)
    return jnp.concatenate([block[:16], tail], axis=1).astype(bf)


def unwire(block, width):
    half = width // 2
    full = block.astype(f32)
    tail = jnp.concatenate([full[:8, width:], full[8:, width:]], axis=1)
    return jnp.concatenate([full[:, :width], tail], axis=0)


def aligned(start, step):
    return pl.multiple_of(start, step)


def body(
    dims,
    lengths_ref,
    q_ref,
    kn_ref,
    vn_ref,
    hidden_ref,
    routes_t_ref,
    gain_ref,
    router_ref,
    k_hbm,
    v_hbm,
    out_hbm,
    gate_hbm,
    up_hbm,
    down_hbm,
    out_ref,
    k_buf,
    v_buf,
    heads,
    hid_out,
    hid_in,
    proj,
    peer,
    resw,
    place_s,
    rank_s,
    put_s,
    stage,
    X,
    first_s,
    other_s,
    rs_s,
    coef_s,
    resid,
    a_s,
    acc_g,
    acc_u,
    active,
    out_w,
    gate_w,
    up_w,
    down_w,
    mine,
    theirs,
    theirs_in,
    y_out,
    y_in,
    zt,
    z_out,
    z_in,
    final,
    kv_sem,
    w_sem,
    a_zs,
    a_ys,
    a_r,
    h_s,
    h_r,
    p_s,
    p_r,
    x_zs,
    x_ys,
    x_os,
    x_r,
    c_s,
    c_r,
    ry_s,
    ry_r,
    rz_s,
    rz_r,
    f_s,
    f_r,
):
    T, Z, R, rows, cap = dims
    ZH, RH = Z // 2, R // 2
    D = hidden_ref.shape[1]
    half_d = D // 2
    total = T * rows
    slots = T * cap
    part = Z * cap
    hid = gate_w.shape[1]
    width = out_w.shape[1]
    wide = R * width
    wave_rows = ZH * R * rows
    _, kv_count, places, head_width = k_buf.shape
    group = q_ref.shape[0] // kv_count
    pieces = (rows // GROUP) * kv_count
    piece_width = group * head_width
    tok = lax.axis_index("tok")
    side = lax.axis_index("side")
    z = tok // R
    r = tok % R
    other = 1 - side
    far = jnp.where(z < ZH, 1, -1)
    near_count = jnp.where(z < ZH, z, Z - 1 - z)

    def ro(d):
        return (r + d) % R

    def nearest(k):
        if k == 0:
            return z
        close = (k + 1) // 2
        close_way = -far if k % 2 == 1 else far
        return jnp.where(k <= 2 * near_count, z + close_way * close, z + far * (k - near_count))

    order = [nearest(k) for k in range(Z)]
    waves = [z // ZH, 1 - z // ZH]

    def copy(src, dst, ssem, rsem, t=None, s=None):
        where = {"tok": tok if t is None else t, "side": side if s is None else s}
        return pltpu.make_async_remote_copy(
            src_ref=src,
            dst_ref=dst,
            send_sem=ssem,
            recv_sem=rsem,
            device_id=where,
            device_id_type=pl.DeviceIdType.MESH,
        )

    pending = []

    def start(c, cond=None):
        pending.append((c, cond))
        if cond is None:
            c.start()
        else:
            pl.when(cond)(c.start)

    barrier = pltpu.get_barrier_semaphore()
    for d in range(1, T):
        pl.semaphore_signal(
            barrier,
            inc=1,
            device_id={"tok": (tok + d) % T, "side": side},
            device_id_type=pl.DeviceIdType.MESH,
        )
    pl.semaphore_signal(
        barrier, inc=1, device_id={"tok": tok, "side": other}, device_id_type=pl.DeviceIdType.MESH
    )

    def kv_load(piece):
        h, g = divmod(piece, kv_count)
        at = pl.ds(h * GROUP, GROUP)
        return [
            pltpu.make_async_copy(k_hbm.at[at, g], k_buf.at[at, g], kv_sem.at[0, piece]),
            pltpu.make_async_copy(v_hbm.at[at, g], v_buf.at[at, g], kv_sem.at[1, piece]),
        ]

    kv_loads = [kv_load(piece) for piece in range(pieces)]
    for pair in kv_loads:
        for load in pair:
            load.start()
    loads = [
        pltpu.make_async_copy(out_hbm, out_w, w_sem.at[0]),
        pltpu.make_async_copy(gate_hbm, gate_w, w_sem.at[1]),
        pltpu.make_async_copy(up_hbm, up_w, w_sem.at[2]),
        pltpu.make_async_copy(down_hbm, down_w, w_sem.at[3]),
    ]
    for load in loads:
        load.start()

    scaling = 1.0 / math.sqrt(head_width)
    eye = lax.broadcasted_iota(i32, (rows, rows), 0) == lax.broadcasted_iota(i32, (rows, rows), 1)
    lens = jnp.sum(jnp.where(eye, lengths_ref[...], 0), axis=1, keepdims=True)
    unit = group * CHUNK
    seq_of = lax.rem(lax.broadcasted_iota(i32, (unit, 1), 0), CHUNK)
    cols_at = lax.broadcasted_iota(i32, (unit, CHUNK * places), 1) - seq_of * places
    own_at = lax.broadcasted_iota(i32, (unit, rows * kv_count), 1) - seq_of * kv_count
    low = -1e30
    kn = kn_ref[...]
    vn = vn_ref[...]

    def attend(c, g):
        q = q_ref[g * group : (g + 1) * group, c * CHUNK : (c + 1) * CHUNK, :]
        q = q.astype(f32).reshape(unit, head_width).astype(bf)
        keys = k_buf[c * CHUNK : (c + 1) * CHUNK, g].reshape(CHUNK * places, head_width)
        vals = v_buf[c * CHUNK : (c + 1) * CHUNK, g].reshape(CHUNK * places, head_width)
        dn = (((1,), (1,)), ((), ()))
        s = lax.dot_general(q, keys, dn, preferred_element_type=f32) * scaling
        so = lax.dot_general(q, kn, dn, preferred_element_type=f32) * scaling
        size = jnp.concatenate([lens[c * CHUNK : (c + 1) * CHUNK]] * group, axis=0)
        s = jnp.where((cols_at >= 0) & (cols_at < size), s, low)
        so = jnp.where(own_at == c * CHUNK * kv_count + g, so, low)
        top = jnp.maximum(
            jnp.max(s, axis=1, keepdims=True), jnp.max(so, axis=1, keepdims=True)
        )
        w = jnp.exp(s - top)
        wo = jnp.exp(so - top)
        inv = 1.0 / (jnp.sum(w, axis=1, keepdims=True) + jnp.sum(wo, axis=1, keepdims=True))
        o = jnp.dot((w * inv).astype(bf), vals, preferred_element_type=f32)
        return o + jnp.dot((wo * inv).astype(bf), vn, preferred_element_type=f32)

    def slot1(t, piece):
        h, g = divmod(piece, kv_count)
        return heads.at[
            pl.ds(aligned(t * rows + h * GROUP, GROUP), GROUP),
            pl.ds(g * piece_width, piece_width),
        ]

    def along(zs, way, piece):
        here = slot1(zs * R + r, piece)
        c = copy(
            here,
            here,
            a_zs.at[(way + 1) // 2, zs, piece],
            a_r.at[zs * R + r, piece],
            t=lax.rem(z + way + Z, Z) * R + r,
        )
        start(c, (z + way >= 0) & (z + way < Z))

    def across(zs, piece):
        here = slot1(zs * R + r, piece)
        for e in range(1, R):
            start(
                copy(
                    here,
                    here,
                    a_ys.at[e, zs, piece],
                    a_r.at[zs * R + r, piece],
                    t=z * R + ro(e),
                )
            )

    def landed1(t, piece):
        here = slot1(t, piece)
        copy(here, here, a_r.at[t, piece], a_r.at[t, piece]).wait_recv()

    home = r // RH == side

    for piece in range(pieces):
        h, g = divmod(piece, kv_count)
        for load in kv_loads[piece]:
            load.wait()
        halves = [attend(c, g) for c in range(h * GROUP // CHUNK, (h + 1) * GROUP // CHUNK)]
        at = pl.ds(aligned(tok * rows + h * GROUP, GROUP), GROUP)
        for k in range(group):
            block = jnp.concatenate([o[k * CHUNK : (k + 1) * CHUNK] for o in halves], axis=0)
            col = (g * group + k) * head_width
            heads[at, col : col + head_width] = block.astype(bf)
        if piece == 0:
            pl.semaphore_wait(barrier, T)
        for way in (1, -1):
            along(z, way, piece)
        across(z, piece)

    for t in range(T):
        hid_out[t] = hidden_ref[:, t * width : (t + 1) * width]

    @pl.when(home)
    def _():
        hid_in[tok] = hid_out[tok]

    for d in range(1, T):
        t = (tok + d) % T
        start(copy(hid_out.at[t], hid_in.at[tok], h_s.at[d], h_r.at[tok], t=t), home)

    resw[...] = jnp.zeros_like(resw)
    lanes = lax.broadcasted_iota(i32, (1, total), 1)
    block_of = lax.div(lanes, rows)
    route0 = routes_t_ref[0:1, :]
    route1 = routes_t_ref[1:2, :]
    erow = lax.broadcasted_iota(i32, (8, total), 0)
    hit8 = (route0 == erow) | (route1 == erow)
    row_i = lax.broadcasted_iota(i32, (total, total), 0)
    col_i = lax.broadcasted_iota(i32, (total, total), 1)
    before = (row_i < col_i) & (lax.div(row_i, rows) == lax.div(col_i, rows))
    rank8 = jnp.dot(
        jnp.where(hit8, 1.0, 0.0).astype(bf),
        jnp.where(before, 1.0, 0.0).astype(bf),
        preferred_element_type=f32,
    ).astype(i32)
    rank_s[...] = rank8
    zs_of = lax.div(block_of, R)
    place_s[...] = jnp.where(hit8 & (rank8 < cap), lax.rem(zs_of, ZH) * cap + rank8, -1)
    wave_lane_r = lax.rem(
        lax.div(lax.broadcasted_iota(i32, (1, wave_rows), 1), rows), R
    )
    wave_row = lax.broadcasted_iota(i32, (ZH * cap, wave_rows), 0)
    for i, w in enumerate(waves):
        placed = place_s[:, pl.ds(aligned(w * wave_rows, wave_rows), wave_rows)]
        for j in range(RH):
            fits = wave_lane_r == side * RH + j
            for e in range(Z):
                want = jnp.where(fits, placed[e : e + 1], -1)
                put_s[i, j, e * ZH * cap : (e + 1) * ZH * cap, :] = jnp.where(
                    wave_row == want, 1.0, 0.0
                ).astype(bf)
    my_rank = rank_s[pl.ds(z, 1), :]
    my_hit = (route0 == z) | (route1 == z)
    target = jnp.where(
        my_hit & (my_rank < cap), (lax.rem(block_of, R) * Z + zs_of) * cap + my_rank, -1
    )
    code = (route0 + route1 - z).astype(f32) + jnp.where(route0 == z, 16.0, 0.0)
    codes = jnp.sum(
        jnp.where(lax.broadcasted_iota(i32, (slots, total), 0) == target, code, 0.0),
        axis=1,
        keepdims=True,
    )
    is_first = jnp.where(codes >= 16.0, 1.0, 0.0)
    first_s[...] = jnp.broadcast_to(is_first, first_s.shape)
    other_s[...] = jnp.broadcast_to((codes - 16.0 * is_first).astype(i32), other_s.shape)

    def xslot(t, rp, w):
        return X.at[t, rp, w]

    def x_across(zs, j, w):
        t, rp = zs * R + r, side * RH + j
        for e in range(1, R):
            start(
                copy(
                    xslot(t, rp, w),
                    xslot(t, rp, w),
                    x_ys.at[e, zs, j, w],
                    x_r.at[t, rp, w],
                    t=z * R + ro(e),
                )
            )

    def x_over(t, j, w):
        rp = side * RH + j
        start(
            copy(
                xslot(t, rp, w), xslot(t, rp, w), x_os.at[t, j, w], x_r.at[t, rp, w], s=other
            )
        )

    def x_landed(t, rp, w):
        copy(xslot(t, rp, w), xslot(t, rp, w), x_r.at[t, rp, w], x_r.at[t, rp, w]).wait_recv()

    def project(i):
        w = waves[i]
        p = jnp.dot(
            heads[pl.ds(aligned(w * wave_rows, wave_rows), wave_rows), :],
            out_w[...],
            preferred_element_type=f32,
        )
        proj[i] = p.reshape(ZH, 2, RH * rows, width)
        c = copy(proj.at[i, :, other], peer.at[i], p_s.at[i], p_r.at[i], s=other)
        start(c)
        for zl in range(ZH):
            for j in range(RH):
                b = (w * ZH + zl) * R + side * RH + j

                @pl.when(b != tok)
                def _(b=b):
                    copy(hid_in.at[b], hid_in.at[b], h_r.at[b], h_r.at[b]).wait_recv()

        c.wait_recv()
        for zl in range(ZH):
            b0 = (w * ZH + zl) * R + side * RH
            whole = (
                proj[i, zl, side]
                + peer[i, zl]
                + hid_in[pl.ds(b0, RH)].astype(f32).reshape(RH * rows, width)
            )
            resw[zl, pl.ds(side * RH, RH)] = whole.astype(bf).reshape(RH, rows, width)
        for j in range(RH):
            packed = jnp.dot(
                put_s[i, j],
                resw[...].reshape(wave_rows, width),
                preferred_element_type=f32,
            )
            stage[i, j] = packed.astype(bf).reshape(Z, ZH * cap, width)
            rp = side * RH + j
            X[tok, rp, w] = stage[i, j, z]
            x_across(z, j, w)
            for k in range(1, Z):
                zd = order[k]
                start(
                    copy(
                        stage.at[i, j, zd],
                        xslot(tok, rp, w),
                        x_zs.at[i, j, zd],
                        x_r.at[tok, rp, w],
                        t=zd * R + r,
                    )
                )
            x_over(tok, j, w)

    loads[0].wait()
    for k in range(1, Z):
        zs = order[k]
        way = jnp.where(zs < z, 1, -1)
        for piece in range(pieces):
            landed1(zs * R + r, piece)
            along(zs, way, piece)
            across(zs, piece)
        last = order[k - 1]
        for e in range(1, R):
            for piece in range(pieces):
                landed1(last * R + ro(e), piece)
        if k == ZH:
            project(0)
    for e in range(1, R):
        for piece in range(pieces):
            landed1(order[Z - 1] * R + ro(e), piece)
    project(1)

    loads[1].wait()
    loads[2].wait()
    tile = min(HIDDEN_TILE, hid)
    squares = jnp.zeros((slots, 1), f32)
    logits = jnp.zeros((slots, Z), f32)

    def spread(ref, n):
        return jnp.concatenate([ref[...]] * (n // 128), axis=1)

    def absorb(zs, idx, squares, logits):
        for r2 in range(R):
            for rp in range(RH):
                for w in range(2):
                    x_landed(zs * R + r2, other * RH + rp, w)
        x = jnp.concatenate(
            [X[zs * R + r2].reshape(slots, width) for r2 in range(R)], axis=1
        ).astype(f32)
        cols = pl.ds(aligned(zs * wide, wide), wide)
        squares = squares + jnp.sum(x * x, axis=1, keepdims=True)
        a = (x * gain_ref[:, cols]).astype(bf)
        a_s[...] = a
        resid[:, cols] = (x * spread(first_s, wide)).astype(bf)
        left = router_ref[:, cols]
        for _ in range(3):
            now = left.astype(bf)
            left = left - now.astype(f32)
            logits = logits + lax.dot_general(
                a, now, (((1,), (1,)), ((), ())), preferred_element_type=f32
            )
        if idx == Z - 1:
            rs = lax.rsqrt(squares / D + 1e-05)
            rs_s[...] = jnp.broadcast_to(rs, rs_s.shape)

        @pl.loop(0, hid // tile)
        def _(n):
            here = pl.ds(aligned(n * tile, tile), tile)
            g = jnp.dot(a_s[...], gate_w[cols, here], preferred_element_type=f32)
            u = jnp.dot(a_s[...], up_w[cols, here], preferred_element_type=f32)
            if idx > 0:
                g = acc_g[:, here] + g
                u = acc_u[:, here] + u
            if idx < Z - 1:
                acc_g[:, here] = g
                acc_u[:, here] = u
            else:
                scale = spread(rs_s, tile)
                g = g * scale
                u = u * scale
                active[:, here] = (g / (1.0 + jnp.exp(-g)) * u).astype(bf)

        return squares, logits

    for k in range(1, Z + 1):
        if k < Z:
            zs = order[k]
            lead = zs // ZH
            for w in (lead, 1 - lead):
                for j in range(RH):
                    x_landed(zs * R + r, side * RH + j, w)
                    x_across(zs, j, w)
                    x_over(zs * R + r, j, w)
        last = order[k - 1]
        lead = last // ZH
        for e in range(1, R):
            for w in (lead, 1 - lead):
                for j in range(RH):
                    x_landed(last * R + ro(e), side * RH + j, w)
                    x_over(last * R + ro(e), j, w)
        squares, logits = absorb(last, k - 1, squares, logits)

    logits = logits * rs_s[:, :1]
    elane = lax.broadcasted_iota(i32, (slots, Z), 1)
    l_self = jnp.sum(jnp.where(elane == z, logits, 0.0), axis=1, keepdims=True)
    l_other = jnp.sum(jnp.where(elane == other_s[:, :Z], logits, 0.0), axis=1, keepdims=True)
    coef_s[...] = jnp.broadcast_to(1.0 / (1.0 + jnp.exp(l_other - l_self)), coef_s.shape)

    loads[3].wait()
    strip = half_d // STRIPS
    own_part = pl.ds(aligned(r * part, part), part)

    def down(start_at, q):
        at = pl.ds(aligned(start_at * half_d + q * strip, 128), strip)
        return jnp.dot(active[...], down_w[:, at], preferred_element_type=f32)

    def y_copy(q, e):
        i = (q, e)
        return copy(y_out.at[i], y_in.at[i], ry_s.at[i], ry_r.at[i], t=z * R + ro(e))

    for q in range(STRIPS):
        theirs[q] = down(other, q).astype(bf)
        c = copy(theirs.at[q], theirs_in.at[q], c_s.at[q], c_r.at[q], s=other)
        start(c)
        mine[q] = down(side, q)
        c.wait_recv()
        mine[q] = (mine[q] + theirs_in[q].astype(f32)) * spread(coef_s, strip)
        for e in range(1, R):
            at = pl.ds(aligned(ro(e) * part, part), part)
            y_out[q, e] = mine[q, at, :].astype(bf)
            start(y_copy(q, e))

    lane_t = lax.broadcasted_iota(i32, (rows, total), 1)
    at_own = lane_t == tok * rows + lax.broadcasted_iota(i32, (rows, total), 0)
    r0 = jnp.sum(jnp.where(at_own, route0, 0), axis=1, keepdims=True)
    r1 = jnp.sum(jnp.where(at_own, route1, 0), axis=1, keepdims=True)
    lane = lax.broadcasted_iota(i32, (rows, 128), 1)
    both = jnp.where((lane == r0) | (lane == r1), 1.0, 0.0).astype(bf)
    row_n = lax.broadcasted_iota(i32, (rows, rows), 0)
    col_n = lax.broadcasted_iota(i32, (rows, rows), 1)
    ranks = jnp.dot(
        jnp.where(col_n < row_n, 1.0, 0.0).astype(bf), both, preferred_element_type=f32
    ).astype(i32)
    at_part = lax.broadcasted_iota(i32, (rows, part), 1)

    def find(k):
        rank = jnp.sum(jnp.where(lane == k, ranks, 0), axis=1, keepdims=True)
        return at_part == k * cap + rank

    pick = jnp.where(find(r0) | find(r1), 1.0, 0.0).astype(bf)

    for q in range(STRIPS):
        cols = pl.ds(aligned(side * half_d + q * strip, 128), strip)
        rows_sum = mine[q, own_part, :] + resid[own_part, cols].astype(f32)
        for e in range(1, R):
            y_copy(q, e).wait_recv()
            rows_sum = rows_sum + y_in[q, e].astype(f32)
        zt[...] = rows_sum
        for k in range(Z):
            to = jnp.where(z < ZH, Z - 1 - k, k)
            z_out[q, to] = wire(zt[pl.ds(aligned(to * cap, 8), cap), :])
            c = copy(
                z_out.at[q, to],
                z_in.at[q, z],
                rz_s.at[q, to],
                rz_r.at[q, z],
                t=to * R + r,
            )
            start(c, to != z)

            @pl.when(to == z)
            def _(q=q, to=to):
                z_in[q, z] = z_out[q, to]

    for q in range(STRIPS):
        for d in range(1, Z):
            src = lax.rem(z + d, Z)
            here = z_in.at[q, src]
            copy(here, here, rz_r.at[q, src], rz_r.at[q, src]).wait_recv()
        got = jnp.concatenate([unwire(z_in[q, e], strip) for e in range(Z)], axis=0)
        done = jnp.dot(pick, got.astype(bf), preferred_element_type=f32).astype(bf)
        final[side, q] = done
        here = final.at[side, q]
        start(copy(here, here, f_s.at[q], f_r.at[q], s=other))
    for q in range(STRIPS):
        there = final.at[other, q]
        copy(there, there, f_r.at[q], f_r.at[q]).wait_recv()
    for s in range(2):
        for q in range(STRIPS):
            out_ref[:, s * half_d + q * strip : s * half_d + (q + 1) * strip] = final[s, q]
    for c, cond in pending:
        if cond is None:
            c.wait_send()
        else:
            pl.when(cond)(c.wait_send)


def local(
    hidden_in,
    queries,
    key_new,
    value_new,
    cache_keys,
    cache_values,
    lengths,
    out_weight,
    norm_gain,
    router_weight,
    gate_weight,
    up_weight,
    down_weight,
    routes,
):
    rows, D = hidden_in.shape
    _, head_count, head_width = queries.shape
    kv_count = key_new.shape[1]
    T = lax.axis_size("tok")
    Z = router_weight.shape[1]
    R = T // Z
    ZH, RH = Z // 2, R // 2
    cap = min(CAP, rows)
    slots = T * cap
    part = Z * cap
    hid = gate_weight.shape[1]
    width = out_weight.shape[1]
    wave_rows = ZH * R * rows
    pieces = (rows // GROUP) * kv_count
    half_d = D // 2
    strip = half_d // STRIPS
    wire_width = strip * cap // 16
    dma = pltpu.SemaphoreType.DMA
    vmem = pl.BlockSpec(memory_space=pltpu.VMEM)
    anyspace = pl.BlockSpec(memory_space=pl.ANY)
    return pl.pallas_call(
        functools.partial(body, (T, Z, R, rows, cap)),
        out_shape=jax.ShapeDtypeStruct((rows, D), bf),
        in_specs=[vmem] * 8 + [anyspace] * 6,
        out_specs=vmem,
        scratch_shapes=[
            pltpu.VMEM(cache_keys.shape, bf),
            pltpu.VMEM(cache_values.shape, bf),
            pltpu.VMEM((T * rows, head_count * head_width), bf),
            pltpu.VMEM((T, rows, width), bf),
            pltpu.VMEM((T, rows, width), bf),
            pltpu.VMEM((2, ZH, 2, RH * rows, width), f32),
            pltpu.VMEM((2, ZH, RH * rows, width), f32),
            pltpu.VMEM((ZH, R, rows, width), bf),
            pltpu.VMEM((8, T * rows), i32),
            pltpu.VMEM((8, T * rows), i32),
            pltpu.VMEM((2, RH, Z * ZH * cap, wave_rows), bf),
            pltpu.VMEM((2, RH, Z, ZH * cap, width), bf),
            pltpu.VMEM((T, R, 2, ZH * cap, width), bf),
            pltpu.VMEM((slots, 128), f32),
            pltpu.VMEM((slots, 128), i32),
            pltpu.VMEM((slots, 128), f32),
            pltpu.VMEM((slots, 128), f32),
            pltpu.VMEM((slots, D), bf),
            pltpu.VMEM((slots, R * width), bf),
            pltpu.VMEM((slots, hid), f32),
            pltpu.VMEM((slots, hid), f32),
            pltpu.VMEM((slots, hid), bf),
            pltpu.VMEM(out_weight.shape, bf),
            pltpu.VMEM(gate_weight.shape, bf),
            pltpu.VMEM(up_weight.shape, bf),
            pltpu.VMEM(down_weight.shape, bf),
            pltpu.VMEM((STRIPS, slots, strip), f32),
            pltpu.VMEM((STRIPS, slots, strip), bf),
            pltpu.VMEM((STRIPS, slots, strip), bf),
            pltpu.VMEM((STRIPS, R, part, strip), bf),
            pltpu.VMEM((STRIPS, R, part, strip), bf),
            pltpu.VMEM((part, strip), f32),
            pltpu.VMEM((STRIPS, Z, 16, wire_width), bf),
            pltpu.VMEM((STRIPS, Z, 16, wire_width), bf),
            pltpu.VMEM((2, STRIPS, rows, strip), bf),
            dma((2, pieces)),
            dma((4,)),
            dma((2, Z, pieces)),
            dma((R, Z, pieces)),
            dma((T, pieces)),
            dma((T,)),
            dma((T,)),
            dma((2,)),
            dma((2,)),
            dma((2, RH, Z)),
            dma((R, Z, RH, 2)),
            dma((T, RH, 2)),
            dma((T, R, 2)),
            dma((STRIPS,)),
            dma((STRIPS,)),
            dma((STRIPS, R)),
            dma((STRIPS, R)),
            dma((STRIPS, Z)),
            dma((STRIPS, Z)),
            dma((STRIPS,)),
            dma((STRIPS,)),
        ],
        compiler_params=pltpu.CompilerParams(
            collective_id=0, has_side_effects=True, vmem_limit_bytes=67043328
        ),
    )(
        lengths.reshape(1, rows),
        jnp.transpose(queries, (1, 0, 2)),
        key_new.reshape(rows * kv_count, head_width),
        value_new.reshape(rows * kv_count, head_width),
        hidden_in,
        routes.T,
        norm_gain.reshape(1, D),
        router_weight.T,
        cache_keys,
        cache_values,
        out_weight,
        gate_weight,
        up_weight,
        down_weight,
    )


def solution(mesh):
    return jax.shard_map(
        local,
        mesh=mesh,
        in_specs=(
            P(("grp", "tok"), None),
            P(("grp", "tok"), "side", None),
            P(("grp", "tok"), "side", None),
            P(("grp", "tok"), "side", None),
            P(("grp", "tok"), "side", None, None),
            P(("grp", "tok"), "side", None, None),
            P(("grp", "tok")),
            P("side", "tok"),
            P(),
            P(),
            P(None, ("tok", "side")),
            P(None, ("tok", "side")),
            P(("tok", "side"), None),
            P("grp", None),
        ),
        out_specs=P(("grp", "tok"), None),
        check_vma=False,
    )
```

time: 72.2 us -> 70.7 us (0.979)
  Pallas kernels: 62.7 us -> 69 us
  matrix products: 4.77 us -> 0 us
  other arithmetic: 1.96 us -> 0 us
  local copies, waits for them, and re-layouts: 2.39 us -> 1.62 us
    pallas_call x1, Pallas kernels: 62.7 us -> 69 us  [local(): pl.pallas_call(functools.partial(body, (T, Z, R, rows, cap)), out_shape=j...]
    dot_general x3 -> x0, matrix products: 4.77 us -> none  [the longest x1 2.95 us: attend(): jnp.einsum('skgd,skpd->skgp', grouped, cache_keys, preferred_element_type...]
    lt x1 -> x0, other arithmetic: 0.88 us -> none  [attend(): usable = jnp.arange(places, dtype=jnp.int32)[None, :] < lengths[:, None]]
    reshape x1 -> x0, local copies, waits for them, and re-layouts: 0.77 us -> none  [attend(): mixture.astype(jnp.bfloat16).reshape(seq_count, head_count * head_width)]
    convert_element_type x1 -> x0, other arithmetic: 0.73 us -> none  [attend(): value_new.astype(jnp.float32)[:, :, None, :]]
    unnamed x3 -> x1, local copies, waits for them, and re-layouts: 1.62 us -> 1.62 us
where the time goes in v1:
time: 70.7 us; the launch traced here: 70.6 us
  Pallas kernels  69 us (98%)
  local copies, waits for them, and re-layouts  1.62 us (2%)
    pallas_call x1, Pallas kernels, local(): pl.pallas_call(functools.partial(body, (T, Z, R, rows, cap)), out_shape=j...  69 us
    unnamed x1, local copies, waits for them, and re-layouts  1.62 us

profile of v1, /device:TPU:0, one launch (start us, length us, event | category | flops | bytes accessed | tf_op | source)
XLA Modules:
  0.0 70.6 jit_solution(12215912400172929479)
XLA Ops:
  0.0 69.0 %shard_map.136 = bf16[32,3072]{1,0:T(8,128)(2,1)} custom-call(s32[1,32]{1,0:T(1,128)} %bitcast.13, bf16[12,32,128]{2,1,0:T(8,128)(2,1)} %bitcast.7, bf16[64,128]{1,0:T(8,128)(2,1)} %bitcast.9, bf16[64,128]{1,0:T(8,128)(2,1)} %bitcast.10, bf16[32,3072]{1,0:T(8,128)(2,1)} %hidden_ref.1, s32[2,256]{1,0:T(2,128)} %bitcast.12, f32[1,3072]{1,0:T(1,128)} %bitcast.11, ...), custom_call_target="tpu_custom_call" | custom-call | tf_op jit(solution)/shard_map/pallas_call | solution.py:639
  69.0 1.6 %copy.16 = bf16[32,3072]{1,0:T(8,128)(2,1)} copy(bf16[32,3072]{1,0:T(8,128)(2,1)} %shard_map.136) | data formatting | bytes 393216

commit v2 on v1

--- a/solution.py
+++ b/solution.py
@@ -83,12 +83,12 @@
     theirs_in,
     y_out,
     y_in,
-    zt,
     z_out,
     z_in,
     final,
     kv_sem,
     w_sem,
+    hello,
     a_zs,
     a_ys,
     a_r,
@@ -129,21 +129,11 @@
     z = tok // R
     r = tok % R
     other = 1 - side
-    far = jnp.where(z < ZH, 1, -1)
-    near_count = jnp.where(z < ZH, z, Z - 1 - z)
-
     def ro(d):
         return (r + d) % R
 
-    def nearest(k):
-        if k == 0:
-            return z
-        close = (k + 1) // 2
-        close_way = -far if k % 2 == 1 else far
-        return jnp.where(k <= 2 * near_count, z + close_way * close, z + far * (k - near_count))
-
-    order = [nearest(k) for k in range(Z)]
-    waves = [z // ZH, 1 - z // ZH]
+    order = [jnp.where(k <= z, z - k, k) for k in range(Z)]
+    waves = [0, 1]
 
     def copy(src, dst, ssem, rsem, t=None, s=None):
         where = {"tok": tok if t is None else t, "side": side if s is None else s}
@@ -166,16 +156,27 @@
             pl.when(cond)(c.start)
 
     barrier = pltpu.get_barrier_semaphore()
-    for d in range(1, T):
+
+    def greet(t, s):
         pl.semaphore_signal(
             barrier,
             inc=1,
-            device_id={"tok": (tok + d) % T, "side": side},
+            device_id={"tok": t, "side": s},
             device_id_type=pl.DeviceIdType.MESH,
         )
-    pl.semaphore_signal(
-        barrier, inc=1, device_id={"tok": tok, "side": other}, device_id_type=pl.DeviceIdType.MESH
-    )
+
+    @pl.when(z > 0)
+    def _():
+        greet(tok - R, side)
+
+    @pl.when(z < Z - 1)
+    def _():
+        greet(tok + R, side)
+
+    for e in range(1, R):
+        greet(z * R + ro(e), side)
+    greet(tok, other)
+    neighbours = R + jnp.where(z > 0, 1, 0) + jnp.where(z < Z - 1, 1, 0)
 
     def kv_load(piece):
         h, g = divmod(piece, kv_count)
@@ -195,8 +196,6 @@
         pltpu.make_async_copy(up_hbm, up_w, w_sem.at[2]),
         pltpu.make_async_copy(down_hbm, down_w, w_sem.at[3]),
     ]
-    for load in loads:
-        load.start()
 
     scaling = 1.0 / math.sqrt(head_width)
     eye = lax.broadcasted_iota(i32, (rows, rows), 0) == lax.broadcasted_iota(i32, (rows, rows), 1)
@@ -236,16 +235,33 @@
             pl.ds(g * piece_width, piece_width),
         ]
 
-    def along(zs, way, piece):
-        here = slot1(zs * R + r, piece)
-        c = copy(
-            here,
-            here,
-            a_zs.at[(way + 1) // 2, zs, piece],
-            a_r.at[zs * R + r, piece],
-            t=lax.rem(z + way + Z, Z) * R + r,
+    def along(to, piece, cond):
+        here = slot1(tok, piece)
+        to = lax.rem(to + Z, Z)
+        start(copy(here, here, a_zs.at[to, piece], a_r.at[tok, piece], t=to * R + r), cond)
+
+    def tell(way):
+        pl.semaphore_signal(
+            hello.at[(1 - way) // 2],
+            inc=1,
+            device_id={"tok": tok + way * R, "side": side},
+            device_id_type=pl.DeviceIdType.MESH,
         )
-        start(c, (z + way >= 0) & (z + way < Z))
+
+    def reach(n):
+        for way in (1, -1):
+            to = z + way * (n + 1)
+
+            @pl.when((to >= 0) & (to < Z))
+            def _(way=way):
+                pl.semaphore_wait(hello.at[(1 + way) // 2], 1)
+
+                @pl.when((z - way >= 0) & (z - way < Z))
+                def _():
+                    tell(-way)
+
+            for piece in range(pieces):
+                along(to, piece, (to >= 0) & (to < Z))
 
     def across(zs, piece):
         here = slot1(zs * R + r, piece)
@@ -270,6 +286,9 @@
         h, g = divmod(piece, kv_count)
         for load in kv_loads[piece]:
             load.wait()
+        if piece == pieces - 1:
+            for load in loads:
+                load.start()
         halves = [attend(c, g) for c in range(h * GROUP // CHUNK, (h + 1) * GROUP // CHUNK)]
         at = pl.ds(aligned(tok * rows + h * GROUP, GROUP), GROUP)
         for k in range(group):
@@ -277,10 +296,16 @@
             col = (g * group + k) * head_width
             heads[at, col : col + head_width] = block.astype(bf)
         if piece == 0:
-            pl.semaphore_wait(barrier, T)
+            pl.semaphore_wait(barrier, neighbours)
+            inner = (z > 0) & (z < Z - 1)
+            for way in (1, -1):
+                pl.when(inner)(functools.partial(tell, way))
         for way in (1, -1):
-            along(z, way, piece)
+            along(z + way, piece, (z + way >= 0) & (z + way < Z))
         across(z, piece)
+
+    if Z > 2:
+        reach(1)
 
     for t in range(T):
         hid_out[t] = hidden_ref[:, t * width : (t + 1) * width]
@@ -289,9 +314,11 @@
     def _():
         hid_in[tok] = hid_out[tok]
 
-    for d in range(1, T):
-        t = (tok + d) % T
-        start(copy(hid_out.at[t], hid_in.at[tok], h_s.at[d], h_r.at[tok], t=t), home)
+    def lend(t):
+        start(copy(hid_out.at[t], hid_in.at[tok], h_s.at[t], h_r.at[tok], t=t), home)
+
+    for e in range(1, R):
+        lend(z * R + ro(e))
 
     resw[...] = jnp.zeros_like(resw)
     lanes = lax.broadcasted_iota(i32, (1, total), 1)
@@ -327,7 +354,9 @@
     my_rank = rank_s[pl.ds(z, 1), :]
     my_hit = (route0 == z) | (route1 == z)
     target = jnp.where(
-        my_hit & (my_rank < cap), (lax.rem(block_of, R) * Z + zs_of) * cap + my_rank, -1
+        my_hit & (my_rank < cap),
+        (lax.rem(block_of, R) * Z + zs_of) * cap + my_rank,
+        -1,
     )
     code = (route0 + route1 - z).astype(f32) + jnp.where(route0 == z, 16.0, 0.0)
     codes = jnp.sum(
@@ -403,46 +432,70 @@
             rp = side * RH + j
             X[tok, rp, w] = stage[i, j, z]
             x_across(z, j, w)
-            for k in range(1, Z):
-                zd = order[k]
-                start(
-                    copy(
-                        stage.at[i, j, zd],
-                        xslot(tok, rp, w),
-                        x_zs.at[i, j, zd],
-                        x_r.at[tok, rp, w],
-                        t=zd * R + r,
-                    )
+            x_over(tok, j, w)
+        for k in range(1, Z):
+            deliver(i, k)
+
+    def deliver(i, k):
+        zd, w = order[k], waves[i]
+        for j in range(RH):
+            rp = side * RH + j
+            start(
+                copy(
+                    stage.at[i, j, zd],
+                    xslot(tok, rp, w),
+                    x_zs.at[i, j, zd],
+                    x_r.at[tok, rp, w],
+                    t=zd * R + r,
                 )
-            x_over(tok, j, w)
+            )
+
+    def relay_z(w, k):
+        zs = order[k]
+        for j in range(RH):
+            x_landed(zs * R + r, side * RH + j, w)
+            x_across(zs, j, w)
+            x_over(zs * R + r, j, w)
+
+    def relay_y(w, k):
+        zs = order[k]
+        for e in range(1, R):
+            for j in range(RH):
+                x_landed(zs * R + ro(e), side * RH + j, w)
+                x_over(zs * R + ro(e), j, w)
 
     loads[0].wait()
+
+    def crossed(zs):
+        for e in range(1, R):
+            for piece in range(pieces):
+                landed1(zs * R + ro(e), piece)
+
     for k in range(1, Z):
         zs = order[k]
-        way = jnp.where(zs < z, 1, -1)
         for piece in range(pieces):
             landed1(zs * R + r, piece)
-            along(zs, way, piece)
             across(zs, piece)
-        last = order[k - 1]
-        for e in range(1, R):
-            for piece in range(pieces):
-                landed1(last * R + ro(e), piece)
-        if k == ZH:
-            project(0)
-    for e in range(1, R):
-        for piece in range(pieces):
-            landed1(order[Z - 1] * R + ro(e), piece)
-    project(1)
-
-    loads[1].wait()
-    loads[2].wait()
+            if piece == 0:
+                lend(zs * R + r)
+                for e in range(1, R):
+                    lend(zs * R + ro(e))
+        if k < Z - 2:
+            reach(k + 1)
+    for w in range(2):
+        for zs in range(w * ZH, (w + 1) * ZH):
+            crossed(zs)
+        project(w)
+    for k in range(1, Z):
+        relay_z(0, k)
+    for k in range(Z):
+        relay_y(0, k)
+
     tile = min(HIDDEN_TILE, hid)
-    squares = jnp.zeros((slots, 1), f32)
-    logits = jnp.zeros((slots, Z), f32)
-
-    def spread(ref, n):
-        return jnp.concatenate([ref[...]] * (n // 128), axis=1)
+    strip = half_d // STRIPS
+
+    def spread(block, n):
+        return jnp.concatenate([block] * (n // 128), axis=1)
 
     def absorb(zs, idx, squares, logits):
         for r2 in range(R):
@@ -456,7 +509,7 @@
         squares = squares + jnp.sum(x * x, axis=1, keepdims=True)
         a = (x * gain_ref[:, cols]).astype(bf)
         a_s[...] = a
-        resid[:, cols] = (x * spread(first_s, wide)).astype(bf)
+        resid[:, cols] = (x * spread(first_s[...], wide)).astype(bf)
         left = router_ref[:, cols]
         for _ in range(3):
             now = left.astype(bf)
@@ -480,60 +533,79 @@
                 acc_g[:, here] = g
                 acc_u[:, here] = u
             else:
-                scale = spread(rs_s, tile)
+                scale = spread(rs_s[...], tile)
                 g = g * scale
                 u = u * scale
                 active[:, here] = (g / (1.0 + jnp.exp(-g)) * u).astype(bf)
 
         return squares, logits
 
-    for k in range(1, Z + 1):
-        if k < Z:
-            zs = order[k]
-            lead = zs // ZH
-            for w in (lead, 1 - lead):
-                for j in range(RH):
-                    x_landed(zs * R + r, side * RH + j, w)
-                    x_across(zs, j, w)
-                    x_over(zs * R + r, j, w)
-        last = order[k - 1]
-        lead = last // ZH
+    def down(which, q):
+        at = pl.ds(aligned(which * half_d + q * strip, 128), strip)
+        return jnp.dot(active[...], down_w[:, at], preferred_element_type=f32)
+
+    def y_copy(q, e):
+        i = (q, e)
+        return copy(y_out.at[i], y_in.at[i], ry_s.at[i], ry_r.at[i], t=z * R + ro(e))
+
+    swaps = []
+
+    def contract(q):
+        theirs[q] = down(other, q).astype(bf)
+        c = copy(theirs.at[q], theirs_in.at[q], c_s.at[q], c_r.at[q], s=other)
+        start(c)
+        swaps.append(c)
+        mine[q] = down(side, q)
+
+    def pass_on(q):
+        swaps[q].wait_recv()
+        mine[q] = (mine[q] + theirs_in[q].astype(f32)) * spread(coef_s[...], strip)
         for e in range(1, R):
-            for w in (lead, 1 - lead):
-                for j in range(RH):
-                    x_landed(last * R + ro(e), side * RH + j, w)
-                    x_over(last * R + ro(e), j, w)
-        squares, logits = absorb(last, k - 1, squares, logits)
-
+            at = pl.ds(aligned(ro(e) * part, part), part)
+            y_out[q, e] = mine[q, at, :].astype(bf)
+            start(y_copy(q, e))
+
+    def send_back(q):
+        own = pl.ds(aligned(r * part, part), part)
+        cols = pl.ds(aligned(side * half_d + q * strip, 128), strip)
+        rows_sum = mine[q, own, :] + resid[own, cols].astype(f32)
+        for e in range(1, R):
+            y_copy(q, e).wait_recv()
+            rows_sum = rows_sum + y_in[q, e].astype(f32)
+        for to in range(Z):
+            z_out[q, to] = wire(rows_sum[to * cap : (to + 1) * cap])
+            c = copy(
+                z_out.at[q, to], z_in.at[q, z], rz_s.at[q, to], rz_r.at[q, z], t=to * R + r
+            )
+            start(c, z != to)
+
+            @pl.when(z == to)
+            def _(q=q, to=to):
+                z_in[q, z] = z_out[q, to]
+
+    squares, logits = jnp.zeros((slots, 1), f32), jnp.zeros((slots, Z), f32)
+    relay_z(1, 1)
+    relay_y(1, 0)
+    for k in range(Z):
+        if k + 2 < Z:
+            relay_z(1, k + 2)
+        if k + 1 < Z:
+            relay_y(1, k + 1)
+        if k == 0:
+            loads[1].wait()
+            loads[2].wait()
+        squares, logits = absorb(order[k], k, squares, logits)
     logits = logits * rs_s[:, :1]
     elane = lax.broadcasted_iota(i32, (slots, Z), 1)
     l_self = jnp.sum(jnp.where(elane == z, logits, 0.0), axis=1, keepdims=True)
     l_other = jnp.sum(jnp.where(elane == other_s[:, :Z], logits, 0.0), axis=1, keepdims=True)
     coef_s[...] = jnp.broadcast_to(1.0 / (1.0 + jnp.exp(l_other - l_self)), coef_s.shape)
-
     loads[3].wait()
-    strip = half_d // STRIPS
-    own_part = pl.ds(aligned(r * part, part), part)
-
-    def down(start_at, q):
-        at = pl.ds(aligned(start_at * half_d + q * strip, 128), strip)
-        return jnp.dot(active[...], down_w[:, at], preferred_element_type=f32)
-
-    def y_copy(q, e):
-        i = (q, e)
-        return copy(y_out.at[i], y_in.at[i], ry_s.at[i], ry_r.at[i], t=z * R + ro(e))
-
     for q in range(STRIPS):
-        theirs[q] = down(other, q).astype(bf)
-        c = copy(theirs.at[q], theirs_in.at[q], c_s.at[q], c_r.at[q], s=other)
-        start(c)
-        mine[q] = down(side, q)
-        c.wait_recv()
-        mine[q] = (mine[q] + theirs_in[q].astype(f32)) * spread(coef_s, strip)
-        for e in range(1, R):
-            at = pl.ds(aligned(ro(e) * part, part), part)
-            y_out[q, e] = mine[q, at, :].astype(bf)
-            start(y_copy(q, e))
+        contract(q)
+        if q > 0:
+            pass_on(q - 1)
+    pass_on(STRIPS - 1)
 
     lane_t = lax.broadcasted_iota(i32, (rows, total), 1)
     at_own = lane_t == tok * rows + lax.broadcasted_iota(i32, (rows, total), 0)
@@ -555,28 +627,7 @@
     pick = jnp.where(find(r0) | find(r1), 1.0, 0.0).astype(bf)
 
     for q in range(STRIPS):
-        cols = pl.ds(aligned(side * half_d + q * strip, 128), strip)
-        rows_sum = mine[q, own_part, :] + resid[own_part, cols].astype(f32)
-        for e in range(1, R):
-            y_copy(q, e).wait_recv()
-            rows_sum = rows_sum + y_in[q, e].astype(f32)
-        zt[...] = rows_sum
-        for k in range(Z):
-            to = jnp.where(z < ZH, Z - 1 - k, k)
-            z_out[q, to] = wire(zt[pl.ds(aligned(to * cap, 8), cap), :])
-            c = copy(
-                z_out.at[q, to],
-                z_in.at[q, z],
-                rz_s.at[q, to],
-                rz_r.at[q, z],
-                t=to * R + r,
-            )
-            start(c, to != z)
-
-            @pl.when(to == z)
-            def _(q=q, to=to):
-                z_in[q, z] = z_out[q, to]
-
+        send_back(q)
     for q in range(STRIPS):
         for d in range(1, Z):
             src = lax.rem(z + d, Z)
@@ -673,13 +724,13 @@
             pltpu.VMEM((STRIPS, slots, strip), bf),
             pltpu.VMEM((STRIPS, R, part, strip), bf),
             pltpu.VMEM((STRIPS, R, part, strip), bf),
-            pltpu.VMEM((part, strip), f32),
             pltpu.VMEM((STRIPS, Z, 16, wire_width), bf),
             pltpu.VMEM((STRIPS, Z, 16, wire_width), bf),
             pltpu.VMEM((2, STRIPS, rows, strip), bf),
             dma((2, pieces)),
             dma((4,)),
-            dma((2, Z, pieces)),
+            pltpu.SemaphoreType.REGULAR((2,)),
+            dma((Z, pieces)),
             dma((R, Z, pieces)),
             dma((T, pieces)),
             dma((T,)),

time: 70.7 us -> 65.9 us (0.932)
  Pallas kernels: 69 us -> 64.1 us
    pallas_call x1, Pallas kernels: 69 us -> 64.1 us  [local(): pl.pallas_call(functools.partial(body, (T, Z, R, rows, cap)), out_shape=j...]
where the time goes in v2:
time: 65.9 us; the launch traced here: 65.8 us
  Pallas kernels  64.1 us (97%)
  local copies, waits for them, and re-layouts  1.62 us (2%)
    pallas_call x1, Pallas kernels, local(): pl.pallas_call(functools.partial(body, (T, Z, R, rows, cap)), out_shape=j...  64.1 us
    unnamed x1, local copies, waits for them, and re-layouts  1.62 us

profile of v2, /device:TPU:0, one launch (start us, length us, event | category | flops | bytes accessed | tf_op | source)
XLA Modules:
  0.0 65.8 jit_solution(1461679577766917786)
XLA Ops:
  0.0 64.1 %shard_map.136 = bf16[32,3072]{1,0:T(8,128)(2,1)} custom-call(s32[1,32]{1,0:T(1,128)} %bitcast.13, bf16[12,32,128]{2,1,0:T(8,128)(2,1)} %bitcast.7, bf16[64,128]{1,0:T(8,128)(2,1)} %bitcast.9, bf16[64,128]{1,0:T(8,128)(2,1)} %bitcast.10, bf16[32,3072]{1,0:T(8,128)(2,1)} %hidden_ref.1, s32[2,256]{1,0:T(2,128)} %bitcast.12, f32[1,3072]{1,0:T(1,128)} %bitcast.11, ...), custom_call_target="tpu_custom_call" | custom-call | tf_op jit(solution)/shard_map/pallas_call | solution.py:690
  64.1 1.6 %copy.16 = bf16[32,3072]{1,0:T(8,128)(2,1)} copy(bf16[32,3072]{1,0:T(8,128)(2,1)} %shard_map.136) | data formatting | bytes 393216

commit v3 on v2

--- a/solution.py
+++ b/solution.py
@@ -9,7 +9,7 @@
 from jax.sharding import PartitionSpec as P
 
 CAP = 24
-HIDDEN_TILE = 512
+HIDDEN_TILE = 2048
 STRIPS = 3
 GROUP = 16
 CHUNK = 8
@@ -37,6 +37,21 @@
 
 def body(
     dims,
+    lengths_hbm,
+    q_hbm,
+    kn_hbm,
+    vn_hbm,
+    hidden_hbm,
+    routes_t_hbm,
+    gain_hbm,
+    router_hbm,
+    k_hbm,
+    v_hbm,
+    out_hbm,
+    gate_hbm,
+    up_hbm,
+    down_hbm,
+    out_ref,
     lengths_ref,
     q_ref,
     kn_ref,
@@ -45,13 +60,7 @@
     routes_t_ref,
     gain_ref,
     router_ref,
-    k_hbm,
-    v_hbm,
-    out_hbm,
-    gate_hbm,
-    up_hbm,
-    down_hbm,
-    out_ref,
+    small_sem,
     k_buf,
     v_buf,
     heads,
@@ -85,11 +94,11 @@
     y_in,
     z_out,
     z_in,
-    final,
     kv_sem,
     w_sem,
     hello,
     a_zs,
+    a_fs,
     a_ys,
     a_r,
     h_s,
@@ -186,10 +195,31 @@
             pltpu.make_async_copy(v_hbm.at[at, g], v_buf.at[at, g], kv_sem.at[1, piece]),
         ]
 
+    smalls = [
+        pltpu.make_async_copy(src, dst, small_sem.at[i])
+        for i, (src, dst) in enumerate(
+            (
+                (lengths_hbm, lengths_ref),
+                (q_hbm, q_ref),
+                (kn_hbm, kn_ref),
+                (vn_hbm, vn_ref),
+                (hidden_hbm, hidden_ref),
+                (routes_t_hbm, routes_t_ref),
+                (gain_hbm, gain_ref),
+                (router_hbm, router_ref),
+            )
+        )
+    ]
+    for load in smalls[:4]:
+        load.start()
     kv_loads = [kv_load(piece) for piece in range(pieces)]
     for pair in kv_loads:
         for load in pair:
             load.start()
+    for load in smalls[4:]:
+        load.start()
+    for load in smalls[:4]:
+        load.wait()
     loads = [
         pltpu.make_async_copy(out_hbm, out_w, w_sem.at[0]),
         pltpu.make_async_copy(gate_hbm, gate_w, w_sem.at[1]),
@@ -237,8 +267,17 @@
 
     def along(to, piece, cond):
         here = slot1(tok, piece)
-        to = lax.rem(to + Z, Z)
+        to = lax.rem(to + 2 * Z, Z)
         start(copy(here, here, a_zs.at[to, piece], a_r.at[tok, piece], t=to * R + r), cond)
+
+    def carry(zs, piece):
+        way = jnp.where(zs < z, 1, -1)
+        here = slot1(zs * R + r, piece)
+        to = lax.rem(z + way + Z, Z)
+        start(
+            copy(here, here, a_fs.at[zs, piece], a_r.at[zs * R + r, piece], t=to * R + r),
+            ((z - zs) * way >= 2) & (z + way >= 0) & (z + way < Z),
+        )
 
     def tell(way):
         pl.semaphore_signal(
@@ -248,20 +287,17 @@
             device_id_type=pl.DeviceIdType.MESH,
         )
 
-    def reach(n):
+    def reach():
         for way in (1, -1):
-            to = z + way * (n + 1)
-
-            @pl.when((to >= 0) & (to < Z))
+            to = z + 2 * way
+            inside = (to >= 0) & (to < Z)
+
+            @pl.when(inside)
             def _(way=way):
                 pl.semaphore_wait(hello.at[(1 + way) // 2], 1)
 
-                @pl.when((z - way >= 0) & (z - way < Z))
-                def _():
-                    tell(-way)
-
             for piece in range(pieces):
-                along(to, piece, (to >= 0) & (to < Z))
+                along(to, piece, inside)
 
     def across(zs, piece):
         here = slot1(zs * R + r, piece)
@@ -304,8 +340,10 @@
             along(z + way, piece, (z + way >= 0) & (z + way < Z))
         across(z, piece)
 
-    if Z > 2:
-        reach(1)
+    reach()
+
+    for load in smalls[4:]:
+        load.wait()
 
     for t in range(T):
         hid_out[t] = hidden_ref[:, t * width : (t + 1) * width]
@@ -475,22 +513,17 @@
         zs = order[k]
         for piece in range(pieces):
             landed1(zs * R + r, piece)
+            if k > 1:
+                carry(zs, piece)
             across(zs, piece)
             if piece == 0:
                 lend(zs * R + r)
                 for e in range(1, R):
                     lend(zs * R + ro(e))
-        if k < Z - 2:
-            reach(k + 1)
     for w in range(2):
         for zs in range(w * ZH, (w + 1) * ZH):
             crossed(zs)
         project(w)
-    for k in range(1, Z):
-        relay_z(0, k)
-    for k in range(Z):
-        relay_y(0, k)
-
     tile = min(HIDDEN_TILE, hid)
     strip = half_d // STRIPS
 
@@ -584,13 +617,17 @@
                 z_in[q, z] = z_out[q, to]
 
     squares, logits = jnp.zeros((slots, 1), f32), jnp.zeros((slots, Z), f32)
-    relay_z(1, 1)
-    relay_y(1, 0)
+    def relay(along_z, k):
+        for w in range(2):
+            (relay_z if along_z else relay_y)(w, k)
+
+    relay(True, 1)
+    relay(False, 0)
     for k in range(Z):
         if k + 2 < Z:
-            relay_z(1, k + 2)
+            relay(True, k + 2)
         if k + 1 < Z:
-            relay_y(1, k + 1)
+            relay(False, k + 1)
         if k == 0:
             loads[1].wait()
             loads[2].wait()
@@ -635,15 +672,12 @@
             copy(here, here, rz_r.at[q, src], rz_r.at[q, src]).wait_recv()
         got = jnp.concatenate([unwire(z_in[q, e], strip) for e in range(Z)], axis=0)
         done = jnp.dot(pick, got.astype(bf), preferred_element_type=f32).astype(bf)
-        final[side, q] = done
-        here = final.at[side, q]
-        start(copy(here, here, f_s.at[q], f_r.at[q], s=other))
+        mid = pl.ds(aligned(side * half_d + q * strip, 128), strip)
+        out_ref[:, mid] = done
+        start(copy(out_ref.at[:, mid], out_ref.at[:, mid], f_s.at[q], f_r.at[q], s=other))
     for q in range(STRIPS):
-        there = final.at[other, q]
-        copy(there, there, f_r.at[q], f_r.at[q]).wait_recv()
-    for s in range(2):
-        for q in range(STRIPS):
-            out_ref[:, s * half_d + q * strip : s * half_d + (q + 1) * strip] = final[s, q]
+        mid = pl.ds(aligned(other * half_d + q * strip, 128), strip)
+        copy(out_ref.at[:, mid], out_ref.at[:, mid], f_r.at[q], f_r.at[q]).wait_recv()
     for c, cond in pending:
         if cond is None:
             c.wait_send()
@@ -689,10 +723,19 @@
     anyspace = pl.BlockSpec(memory_space=pl.ANY)
     return pl.pallas_call(
         functools.partial(body, (T, Z, R, rows, cap)),
-        out_shape=jax.ShapeDtypeStruct((rows, D), bf),
-        in_specs=[vmem] * 8 + [anyspace] * 6,
+        out_shape=pltpu.VMEM((rows, D), bf),
+        in_specs=[anyspace] * 14,
         out_specs=vmem,
         scratch_shapes=[
+            pltpu.VMEM((1, rows), i32),
+            pltpu.VMEM((head_count, rows, head_width), bf),
+            pltpu.VMEM((rows * kv_count, head_width), bf),
+            pltpu.VMEM((rows * kv_count, head_width), bf),
+            pltpu.VMEM((rows, D), bf),
+            pltpu.VMEM((2, T * rows), i32),
+            pltpu.VMEM((1, D), f32),
+            pltpu.VMEM((Z, D), f32),
+            dma((8,)),
             pltpu.VMEM(cache_keys.shape, bf),
             pltpu.VMEM(cache_values.shape, bf),
             pltpu.VMEM((T * rows, head_count * head_width), bf),
@@ -726,10 +769,10 @@
             pltpu.VMEM((STRIPS, R, part, strip), bf),
             pltpu.VMEM((STRIPS, Z, 16, wire_width), bf),
             pltpu.VMEM((STRIPS, Z, 16, wire_width), bf),
-            pltpu.VMEM((2, STRIPS, rows, strip), bf),
             dma((2, pieces)),
             dma((4,)),
             pltpu.SemaphoreType.REGULAR((2,)),
+            dma((Z, pieces)),
             dma((Z, pieces)),
             dma((R, Z, pieces)),
             dma((T, pieces)),
@@ -751,7 +794,7 @@
             dma((STRIPS,)),
         ],
         compiler_params=pltpu.CompilerParams(
-            collective_id=0, has_side_effects=True, vmem_limit_bytes=67043328
+            collective_id=0, has_side_effects=True, vmem_limit_bytes=66600000
         ),
     )(
         lengths.reshape(1, rows),

time: 65.9 us -> 55.2 us (0.84)
  Pallas kernels: 64.1 us -> 54.4 us
  local copies, waits for them, and re-layouts: 1.62 us -> 0.68 us
    pallas_call x1, Pallas kernels: 64.1 us -> 54.4 us  [local(): pl.pallas_call(functools.partial(body, (T, Z, R, rows, cap)), out_shape=p...]
    unnamed x1, local copies, waits for them, and re-layouts: 1.62 us -> 0.68 us
where the time goes in v3:
time: 55.2 us; the launch traced here: 55.1 us
  Pallas kernels  54.4 us (99%)
  local copies, waits for them, and re-layouts  0.68 us (1%)
    pallas_call x1, Pallas kernels, local(): pl.pallas_call(functools.partial(body, (T, Z, R, rows, cap)), out_shape=p...  54.4 us

profile of v3, /device:TPU:0, one launch (start us, length us, event | category | flops | bytes accessed | tf_op | source)
XLA Modules:
  0.0 55.1 jit_solution(7485805519163994112)
XLA Ops:
  0.0 54.4 %shard_map.136 = bf16[32,3072]{1,0:T(8,128)(2,1)S(1)} custom-call(s32[1,32]{1,0:T(1,128)} %bitcast.13, bf16[12,32,128]{2,1,0:T(8,128)(2,1)} %bitcast.7, bf16[64,128]{1,0:T(8,128)(2,1)} %bitcast.9, bf16[64,128]{1,0:T(8,128)(2,1)} %bitcast.10, bf16[32,3072]{1,0:T(8,128)(2,1)} %hidden_hbm.1, s32[2,256]{1,0:T(2,128)} %bitcast.12, f32[1,3072]{1,0:T(1,128)} %bitcast.11, ...), custom_call_target="tpu_custom_call" | custom-call | tf_op jit(solution)/shard_map/pallas_call | solution.py:724
  54.4 0.7 %copy.16 = bf16[32,3072]{1,0:T(8,128)(2,1)} copy(bf16[32,3072]{1,0:T(8,128)(2,1)S(1)} %shard_map.136) | data formatting | bytes 393216

commit v4 on v3

--- a/solution.py
+++ b/solution.py
@@ -142,7 +142,8 @@
         return (r + d) % R
 
     order = [jnp.where(k <= z, z - k, k) for k in range(Z)]
-    waves = [0, 1]
+    top_chip = jnp.where(z == Z - 1, 1, 0)
+    waves = [top_chip, 1 - top_chip]
 
     def copy(src, dst, ssem, rsem, t=None, s=None):
         where = {"tok": tok if t is None else t, "side": side if s is None else s}
@@ -163,6 +164,13 @@
             c.start()
         else:
             pl.when(cond)(c.start)
+
+    def drain(copies):
+        for c, cond in copies:
+            if cond is None:
+                c.wait_send()
+            else:
+                pl.when(cond)(c.wait_send)
 
     barrier = pltpu.get_barrier_semaphore()
 
@@ -287,17 +295,17 @@
             device_id_type=pl.DeviceIdType.MESH,
         )
 
-    def reach():
+    def meet():
+        for way in (1, -1):
+
+            @pl.when((z + 2 * way >= 0) & (z + 2 * way < Z))
+            def _(way=way):
+                pl.semaphore_wait(hello.at[(1 + way) // 2], 1)
+
+    def reach(piece):
         for way in (1, -1):
             to = z + 2 * way
-            inside = (to >= 0) & (to < Z)
-
-            @pl.when(inside)
-            def _(way=way):
-                pl.semaphore_wait(hello.at[(1 + way) // 2], 1)
-
-            for piece in range(pieces):
-                along(to, piece, inside)
+            along(to, piece, (to >= 0) & (to < Z))
 
     def across(zs, piece):
         here = slot1(zs * R + r, piece)
@@ -339,8 +347,12 @@
         for way in (1, -1):
             along(z + way, piece, (z + way >= 0) & (z + way < Z))
         across(z, piece)
-
-    reach()
+        if piece == pieces - 2:
+            meet()
+            for earlier in range(piece):
+                reach(earlier)
+        if piece >= pieces - 2:
+            reach(piece)
 
     for load in smalls[4:]:
         load.wait()
@@ -520,10 +532,10 @@
                 lend(zs * R + r)
                 for e in range(1, R):
                     lend(zs * R + ro(e))
-    for w in range(2):
-        for zs in range(w * ZH, (w + 1) * ZH):
-            crossed(zs)
-        project(w)
+    for i, w in enumerate(waves):
+        for zl in range(ZH):
+            crossed(w * ZH + zl)
+        project(i)
     tile = min(HIDDEN_TILE, hid)
     strip = half_d // STRIPS
 
@@ -588,6 +600,8 @@
         c = copy(theirs.at[q], theirs_in.at[q], c_s.at[q], c_r.at[q], s=other)
         start(c)
         swaps.append(c)
+        if q > 0:
+            pass_on(q - 1)
         mine[q] = down(side, q)
 
     def pass_on(q):
@@ -638,10 +652,9 @@
     l_other = jnp.sum(jnp.where(elane == other_s[:, :Z], logits, 0.0), axis=1, keepdims=True)
     coef_s[...] = jnp.broadcast_to(1.0 / (1.0 + jnp.exp(l_other - l_self)), coef_s.shape)
     loads[3].wait()
+    settled = len(pending)
     for q in range(STRIPS):
         contract(q)
-        if q > 0:
-            pass_on(q - 1)
     pass_on(STRIPS - 1)
 
     lane_t = lax.broadcasted_iota(i32, (rows, total), 1)
@@ -663,6 +676,7 @@
 
     pick = jnp.where(find(r0) | find(r1), 1.0, 0.0).astype(bf)
 
+    drain(pending[:settled])
     for q in range(STRIPS):
         send_back(q)
     for q in range(STRIPS):
@@ -678,11 +692,7 @@
     for q in range(STRIPS):
         mid = pl.ds(aligned(other * half_d + q * strip, 128), strip)
         copy(out_ref.at[:, mid], out_ref.at[:, mid], f_r.at[q], f_r.at[q]).wait_recv()
-    for c, cond in pending:
-        if cond is None:
-            c.wait_send()
-        else:
-            pl.when(cond)(c.wait_send)
+    drain(pending[settled:])
 
 
 def local(

time: 55.2 us -> 55.1 us (level)
  no operation moved by 1% of the time
where the time goes in v4:
time: 55.1 us; the launch traced here: 54.9 us
  Pallas kernels  54.2 us (98%)
  local copies, waits for them, and re-layouts  0.68 us (1%)
    pallas_call x1, Pallas kernels, local(): pl.pallas_call(functools.partial(body, (T, Z, R, rows, cap)), out_shape=p...  54.2 us

profile of v4, /device:TPU:0, one launch (start us, length us, event | category | flops | bytes accessed | tf_op | source)
XLA Modules:
  0.0 54.9 jit_solution(15051255891901100179)
XLA Ops:
  0.0 54.2 %shard_map.136 = bf16[32,3072]{1,0:T(8,128)(2,1)S(1)} custom-call(s32[1,32]{1,0:T(1,128)} %bitcast.13, bf16[12,32,128]{2,1,0:T(8,128)(2,1)} %bitcast.7, bf16[64,128]{1,0:T(8,128)(2,1)} %bitcast.9, bf16[64,128]{1,0:T(8,128)(2,1)} %bitcast.10, bf16[32,3072]{1,0:T(8,128)(2,1)} %hidden_hbm.1, s32[2,256]{1,0:T(2,128)} %bitcast.12, f32[1,3072]{1,0:T(1,128)} %bitcast.11, ...), custom_call_target="tpu_custom_call" | custom-call | tf_op jit(solution)/shard_map/pallas_call | solution.py:734
  54.3 0.7 %copy.16 = bf16[32,3072]{1,0:T(8,128)(2,1)} copy(bf16[32,3072]{1,0:T(8,128)(2,1)S(1)} %shard_map.136) | data formatting | bytes 393216
